TPU v7x, 128 devices: a whole 4x4x4 slice. The times are simulated.
128 devices in a mesh: row: 8 (over z, x_hi), col: 16 (over y, x_lo, core).
Axes of the slice: x: 4 (x_hi: 2, x_lo: 2; x = x_hi * 2 + x_lo), y: 4, z: 4, core: 2. Of those that a mesh axis runs over, the one named last changes fastest.
Arguments:
- node_feats: bfloat16 [16384, 512], P(('row', 'col')), may hold values from -80 to 80
- block_mask: int32 [128, 128], replicated, may hold values from 0 to 1, as said below
- w_qkv: bfloat16 [2, 512, 1536], replicated, may hold values from -0.25 to 0.25
- w_out: bfloat16 [2, 512, 512], replicated, may hold values from -0.79296875 to 0.79296875
- w_up: bfloat16 [2, 512, 1024], replicated, may hold values from -0.25 to 0.25
- w_down: bfloat16 [2, 1024, 512], replicated, may hold values from -0.1875 to 0.1875
- ln_gain: float32 [2, 2, 512], replicated, may hold values from 0.1 to 1.9
- ln_bias: float32 [2, 2, 512], replicated, may hold values from -3 to 3
Outputs:
- nodes_out: bfloat16 [16384, 512], P(('row', 'col'))
Inputs may be any that keep to these rules, and one draw needn't show every extreme that they name: `block_mask`: A symmetric 0/1 table over the 128 node blocks; every block is linked with itself.
All inputs are finite; a program needn't handle non-finite values.
Results may differ from a plain program's by a relative error of at most 0.022.
Values may be sent and summed in bfloat16 or wider, within the bound.
A program may use at most 128 MiB of HBM per device.

v0:
```python
import functools
import math

import jax
import jax.numpy as jnp
from jax import lax
from jax.experimental import pallas as pl
from jax.experimental.pallas import tpu as pltpu
from jax.sharding import PartitionSpec as P

HEADS = 8
F32, BF16 = jnp.float32, jnp.bfloat16
FLOOR = -1e30
MESH = pl.DeviceIdType.MESH
OFFS = (0, -1, 1, 2)
GROUP, AHEAD = 4, 4


def layer_norm(values, gain, bias):
    center = values - jnp.mean(values, axis=-1, keepdims=True)
    spread = jnp.mean(center * center, axis=-1, keepdims=True)
    return center * lax.rsqrt(spread + 1e-05) * gain + bias


def gelu(v):
    inner = math.sqrt(2.0 / math.pi) * (v + 0.044715 * (v * v * v))
    return v * (0.5 * (1.0 + jnp.tanh(inner)))


def coords():
    row, col = lax.axis_index("row"), lax.axis_index("col")
    return (row % 2) * 2 + (col // 2) % 2, col // 4, row // 2, col % 2


def dev(x, y, z, c):
    return {"row": z * 2 + x // 2, "col": y * 4 + (x % 2) * 2 + c}


def exchange(l, first, last, *refs):
    refs = list(refs)
    take = refs.pop
    x_in = take(0)
    if not first:
        pin, sin = take(0), take(0)
    hqkv = None if last else take(0)
    if not first:
        hout, hup, hdown, gain, bias = (take(0) for _ in range(5))
    if last:
        x_out = take(0)
    else:
        kbuf, vbuf, qbuf = take(0), take(0), take(0)
        if not first:
            x_out = take(0)
    w_sem, snd = take(0), take(0)
    if not first:
        wout, wup, wdown, rp, rs, er, tr, own_sem = (take(0) for _ in range(8))
    if not last:
        wk, wv, wq, wvt, wqt, xk, xq, x_sem, ra, rb, rd, ry, rq = (take(0) for _ in range(13))
    assert not refs

    rows, width = x_in.shape
    half = rows // 2
    cols = width // 2
    hd = width // HEADS
    scale = math.log2(math.e) / math.sqrt(hd)
    x, y, z, c = coords()
    e = 1 - c
    a0, b0 = z * e + x * c, x * e + z * c
    av = [a0] + [(a0 + 4 + k) % 4 for k in OFFS[1:]]
    bv = [b0] + [(b0 + 4 + k) % 4 for k in OFFS[1:]]
    yv = [y] + [(y + 4 + k) % 4 for k in OFFS[1:]]
    fa, fb = 4 - 3 * c, 1 + 3 * c
    partner = dev(x, y, z, e)

    def dev_a(i):
        return dev(x * e + av[i] * c, y, av[i] * e + z * c, c)

    def dev_b(i):
        return dev(bv[i] * e + x * c, y, z * e + bv[i] * c, c)

    def dev_y(i, core):
        return dev(x, yv[i], z, core)

    def nat(ka, kb):
        return av[ka] * fa + bv[kb] * fb

    def nat_partner(ka, kb):
        return bv[ka] * fb + av[kb] * fa

    started = []

    def remote(src, dst, send, recv, device):
        return pltpu.make_async_remote_copy(
            src_ref=src, dst_ref=dst, send_sem=send, recv_sem=recv, device_id=device, device_id_type=MESH)

    def go(src, dst, recv, device):
        copy = remote(src, dst, snd.at[len(started)], recv, device)
        copy.start()
        started.append(copy)

    if first:
        own = pltpu.make_async_copy(x_in, xk.at[c * 16 + z * 4 + x], x_sem)
        own.start()
    loads = []
    if not last:
        for i, dst in enumerate((wq, wk, wv)):
            src = hqkv.at[l, :, pl.ds(pl.multiple_of(i * width + c * cols, cols), cols)]
            loads.append(pltpu.make_async_copy(src, dst, w_sem.at[i]))
    if not first:
        for i, (src, dst) in enumerate(((hout, wout), (hup, wup), (hdown, wdown))):
            loads.append(pltpu.make_async_copy(src.at[l - 1], dst, w_sem.at[3 + i]))
    for load in loads:
        load.start()

    barrier = pltpu.get_barrier_semaphore()
    peers = [partner]
    if not last:
        peers += [dev_a(1), dev_a(2), dev_b(1), dev_b(2)]
    if first:
        peers += [dev_y(1, c), dev_y(2, c)]
    else:
        peers += [dev_y(i, core) for i in (1, 2, 3) for core in (0, 1)]
    for peer in peers:
        pl.semaphore_signal(barrier, inc=1, device_id=peer, device_id_type=MESH)
    pl.semaphore_wait(barrier, len(peers))

    if not first:
        def ret(i, core, src_slot):
            go(sin.at[src_slot], rs.at[y, c], tr.at[y, c], dev_y(i, core))
            go(pin.at[src_slot], rp.at[y, c], er.at[y, c], dev_y(i, core))

        for i in (3, 1, 2):
            for core in (0, 1):
                ret(i, core, yv[i] * 2 + core)
        go(sin.at[y * 2 + e], rs.at[y, c], tr.at[y, c], partner)
        go(pin.at[y * 2 + e], rp.at[y, c], er.at[y, c], partner)
        own_s = pltpu.make_async_copy(sin.at[y * 2 + c], rs.at[y, c], own_sem.at[0])
        own_p = pltpu.make_async_copy(pin.at[y * 2 + c], rp.at[y, c], own_sem.at[1])
        own_s.start()
        own_p.start()

    def project_setup():
        if last:
            return
        qbuf[...] = jnp.zeros_like(qbuf)
        n_k = kbuf.shape[0]
        vbuf[:n_k, :, 2 * hd:, :] = jnp.ones((n_k, 2, vbuf.shape[2] - 2 * hd, rows), BF16)
        vbuf[n_k] = jnp.zeros(vbuf.shape[1:], BF16)
        for load in loads[:3]:
            load.wait()
        wqt[...] = wq[...].T
        wvt[...] = wv[...].T

    if not first:
        project_setup()
        for load in loads[0 if last else 3:]:
            load.wait()
        own_s.wait()
        own_p.wait()

        def wait_in(buf, recv, i, core):
            remote(buf.at[yv[i], core], buf.at[yv[i], core], snd.at[0], recv.at[yv[i], core], partner).wait_recv()

        wait_in(rs, tr, 0, e)
        wait_in(rp, er, 0, e)
        for i in (1, 2, 3):
            for core in (0, 1):
                wait_in(rs, tr, i, core)
                wait_in(rp, er, i, core)
        parts = []
        for g in range(2):
            stats = [rs[yv[i], g] for i in range(4)]
            top = functools.reduce(jnp.maximum, [t[:4] for t in stats])
            share = [jnp.exp2(t[:4] - top) for t in stats]
            mass = functools.reduce(jnp.add, [f * t[4:] for f, t in zip(share, stats)])
            inverse = 1.0 / mass
            share = [f * inverse for f in share]
            for h in range(4):
                span = slice(h * hd, (h + 1) * hd)
                total = rp[yv[0], g, span].astype(F32) * share[0][h:h + 1]
                for i in (1, 2, 3):
                    total = total + rp[yv[i], g, span].astype(F32) * share[i][h:h + 1]
                parts.append(total)
        attn = jnp.concatenate(parts, axis=0).T.astype(BF16)
        mixed = jnp.dot(attn, wout[...], preferred_element_type=F32)
        hidden = layer_norm(x_in[...].astype(F32) + mixed,
                            gain[l - 1, 0:1], bias[l - 1, 0:1]).astype(BF16)
        up = gelu(jnp.dot(hidden, wup[...], preferred_element_type=F32)).astype(BF16)
        down = jnp.dot(up, wdown[...], preferred_element_type=F32)
        x_new = layer_norm(hidden.astype(F32) + down, gain[l - 1, 1:2], bias[l - 1, 1:2]).astype(BF16)
        if not last:
            xk[c * 16 + z * 4 + x] = x_new
        x_out[...] = x_new

    if not last:
        own_slot = c * 16 + z * 4 + x
        if first:
            own.wait()

        def part(ref, h):
            return ref if h is None else ref.at[pl.ds(h * half, half)]

        def arrived(ref, recv):
            remote(ref, ref, snd.at[0], recv, partner).wait_recv()

        def send_a(ka, h, up):
            ref = part(xk.at[c * 16 + nat(ka, 0)], h)
            to = (1 if up else 2) if ka == 0 else 3
            go(ref, ref, ra.at[to - 1, h], dev_a(2 if up else 1))

        def wait_a(ka, h):
            arrived(part(xk.at[c * 16 + nat(ka, 0)], h), ra.at[ka - 1, h])

        def send_b(ka, kb, h, up):
            ref = part(xk.at[c * 16 + nat(ka, kb)], h)
            to = (1 if up else 2) if kb == 0 else 3
            go(ref, ref, rb.at[ka, to - 1, h], dev_b(2 if up else 1))

        def wait_b(ka, kb, h):
            arrived(part(xk.at[c * 16 + nat(ka, kb)], h), rb.at[ka, kb - 1, h])

        def send_y(i, h, up):
            ref = part(xk.at[own_slot] if i == 0 else xq.at[c, yv[i]], h)
            to = (1 if up else 2) if i == 0 else 3
            go(ref, part(xq.at[c, yv[i]], h), ry.at[to - 1, h], dev_y(2 if up else 1, c))

        def wait_y(i, h):
            arrived(part(xq.at[c, yv[i]], h), ry.at[i - 1, h])

        def share(ka, kb):
            n = nat(ka, kb)
            go(xk.at[c * 16 + n], xk.at[c * 16 + n], rd.at[n], partner)

        def share_y(i):
            ref = xq.at[c, yv[i]]
            go(ref, ref, rq.at[i - 1], partner)

        def project_kv(s, t):
            xs = jnp.concatenate([xk[s], xk[t]], axis=0)
            k = jnp.dot(xs, wk[...], preferred_element_type=F32).astype(BF16)
            v = lax.dot_general(wvt[...], xs, (((1,), (1,)), ((), ())), preferred_element_type=F32).astype(BF16)
            for i, to in enumerate((s, t)):
                span = slice(i * rows, (i + 1) * rows)
                kbuf[to] = k[span]
                vbuf[to, 0, :2 * hd] = v[:2 * hd, span]
                vbuf[to, 1, :2 * hd] = v[2 * hd:, span]

        def project_q(q, xs):
            t = lax.dot_general(wqt[...], xs, (((1,), (1,)), ((), ())), preferred_element_type=F32)
            t = (t * scale).astype(BF16)
            for h in range(2):
                base = h * 2 * hd
                qbuf[q, h, :hd, :rows] = t[base:base + hd]
                qbuf[q, h, hd:, rows:] = t[base + hd:base + 2 * hd]

        def finish(*blocks):
            for ka, kb in blocks:
                n, m = nat(ka, kb), nat_partner(ka, kb)
                s, t = c * 16 + n, e * 16 + m
                arrived(xk.at[t], rd.at[m])
                project_kv(s, t)

        def finish_y(*which):
            for i in which:
                if i == 0:
                    project_q(y * 2 + c, xk[own_slot])
                    project_q(y * 2 + e, xk[e * 16 + z * 4 + x])
                    continue
                arrived(xq.at[e, yv[i]], rq.at[i - 1])

                @pl.loop(0, 2)
                def _(core):
                    project_q(yv[i] * 2 + core, xq[core, yv[i]])

        for h in (0, 1):
            send_a(0, h, True)
            send_a(0, 1 - h, False)
            send_b(0, 0, h, True)
            send_b(0, 0, 1 - h, False)
            send_y(0, h, True)
            send_y(0, 1 - h, False)
        share(0, 0)
        if first:
            project_setup()
        finish((0, 0))
        finish_y(0)
        wait_a(1, 0)
        send_a(1, 0, True)
        send_b(1, 0, 0, True)
        wait_a(2, 1)
        send_a(2, 1, False)
        send_b(2, 0, 1, False)
        wait_b(0, 1, 0)
        send_b(0, 1, 0, True)
        wait_b(0, 2, 1)
        send_b(0, 2, 1, False)
        wait_y(1, 0)
        send_y(1, 0, True)
        wait_y(2, 1)
        send_y(2, 1, False)
        wait_a(1, 1)
        send_b(1, 0, 1, False)
        wait_a(2, 0)
        send_b(2, 0, 0, True)
        send_b(1, 0, 1, True)
        send_b(1, 0, 0, False)
        send_b(2, 0, 0, False)
        send_b(2, 0, 1, True)
        share(1, 0)
        share(2, 0)
        wait_b(0, 1, 1)
        share(0, 1)
        wait_b(0, 2, 0)
        share(0, 2)
        wait_y(1, 1)
        share_y(1)
        wait_y(2, 0)
        share_y(2)
        finish((1, 0))
        wait_a(3, 0)
        send_b(3, 0, 0, True)
        wait_a(3, 1)
        send_b(3, 0, 1, False)
        send_b(3, 0, 1, True)
        send_b(3, 0, 0, False)
        share(3, 0)
        finish((2, 0), (0, 1))
        for ka in (1, 2):
            wait_b(ka, 1, 0)
            send_b(ka, 1, 0, True)
            wait_b(ka, 2, 1)
            send_b(ka, 2, 1, False)
        wait_b(0, 3, 0)
        wait_b(0, 3, 1)
        share(0, 3)
        finish((0, 2))
        finish_y(1, 2)
        for ka in (1, 2):
            wait_b(ka, 1, 1)
            share(ka, 1)
            wait_b(ka, 2, 0)
            share(ka, 2)
        wait_y(3, 0)
        wait_y(3, 1)
        share_y(3)
        finish((3, 0))
        wait_b(3, 1, 0)
        send_b(3, 1, 0, True)
        wait_b(3, 2, 1)
        send_b(3, 2, 1, False)
        finish((0, 3), (1, 1))
        for ka in (1, 2):
            wait_b(ka, 3, 0)
            wait_b(ka, 3, 1)
            share(ka, 3)
        wait_b(3, 1, 1)
        share(3, 1)
        wait_b(3, 2, 0)
        share(3, 2)
        finish((1, 2), (2, 1), (2, 2))
        finish_y(3)
        finish((1, 3), (2, 3))
        wait_b(3, 3, 0)
        wait_b(3, 3, 1)
        share(3, 3)
        finish((3, 1), (3, 2), (3, 3))

    for copy in started:
        copy.wait_send()


def attend(mask, kbuf, vbuf, qbuf, pout, sout, smask, pairs, sbuf, peak, acc, top, den, sem):
    n_q, n_k, rows = qbuf.shape[0], kbuf.shape[0], kbuf.shape[1]
    hd = qbuf.shape[2] // 2
    x, y, z, c = coords()
    row = lax.axis_index("row")
    load = pltpu.make_async_copy(mask.at[pl.ds(row * 16, 16)], smask, sem)
    load.start()
    acc[...] = jnp.zeros_like(acc)
    den[...] = jnp.zeros_like(den)
    top[...] = jnp.full_like(top, FLOOR)
    load.wait()

    def scan(q, n):
        at = (q // 2) * 4 + (x % 2) * 2 + q % 2
        base = q * 4096
        for s in range(n_k):
            core, zz, xx = s // 16, (s % 16) // 4, s % 4
            kid = (zz * 2 + xx // 2) * 16 + y * 4 + (xx % 2) * 2 + core
            pairs[n] = base + (s * 64 + s)
            n = n + smask[at, kid]
        before = pairs[jnp.maximum(n - 1, 0)]
        pairs[n] = (before // 64) * 64 + n_k
        return n + n % 2

    n = lax.fori_loop(0, n_q, scan, 0)
    for i in range(4 * GROUP):
        pairs[n + i] = n_q * 4096 + n_k

    units = 2 * GROUP

    def scores(it, i):
        d, h = i // 2, i % 2
        code = [pairs[(it * GROUP + d) * 2 + j] for j in range(2)]
        q = jnp.minimum(code[0] // 4096, n_q - 1)
        best = []
        for j in range(2):
            k = (code[j] // 64) % 64
            s = jnp.dot(kbuf[k, :, h * 2 * hd:(h + 1) * 2 * hd], qbuf[q, h], preferred_element_type=F32)
            sbuf[i, j * rows:(j + 1) * rows] = s
            best.append(jnp.max(s, axis=0, keepdims=True))
        peak[i] = jnp.maximum(*best)

    def values(it, i):
        d, h = i // 2, i % 2
        code = [pairs[(it * GROUP + d) * 2 + j] for j in range(2)]
        q = code[0] // 4096
        old = top[q, h]
        new = jnp.maximum(old, peak[i])
        p = jnp.exp2(sbuf[i] - new).astype(BF16)
        v = jnp.concatenate([vbuf[code[j] % 64, h] for j in range(2)], axis=1)
        o = jnp.dot(v, p, preferred_element_type=F32)
        alpha = jnp.exp2(old - new)
        top[q, h] = new
        den[q, h] = den[q, h] * alpha + o[2 * hd:2 * hd + 1]
        for g in range(2):
            lanes = slice(g * rows, (g + 1) * rows)
            span = slice((2 * h + g) * hd, (2 * h + g + 1) * hd)
            acc[q, span] = acc[q, span] * alpha[:, lanes] + o[g * hd:(g + 1) * hd, lanes]

    for i in range(AHEAD):
        scores(0, i)

    @pl.loop(0, (n + 2 * GROUP - 1) // (2 * GROUP))
    def _(it):
        for i in range(units):
            ahead = i + AHEAD
            scores(it + ahead // units, ahead % units)
            values(it, i)

    for q in range(n_q):
        pout[q] = acc[q].astype(BF16)
        for h in range(2):
            for g in range(2):
                lanes = slice(g * rows, (g + 1) * rows)
                sout[q, 2 * h + g:2 * h + g + 1] = top[q, h, :, lanes]
                sout[q, 4 + 2 * h + g:5 + 2 * h + g] = den[q, h, :, lanes]


def solution(mesh):
    def per_device(x, mask, wqkv, wout, wup, wdown, gain, bias):
        rows, width = x.shape
        layers = wqkv.shape[0]
        cols = width // 2
        ff = wup.shape[2]
        hd = width // HEADS
        n_q, n_k = 8, 32
        vmem, any_ = pl.BlockSpec(memory_space=pltpu.VMEM), pl.BlockSpec(memory_space=pltpu.HBM)
        dma = pltpu.SemaphoreType.DMA
        shape = jax.ShapeDtypeStruct
        proj = [shape((n_k, rows, cols), BF16), shape((n_k + 1, 2, 2 * hd + 16, rows), BF16),
                shape((n_q, 2, 2 * hd, 2 * rows), BF16)]

        def call_exchange(l, x, part):
            first, last = l == 0, l == layers
            ins, specs, outs = [x], [any_ if first else vmem], []
            if not first:
                ins += part
                specs += [vmem, vmem]
            if not last:
                ins.append(wqkv)
                specs.append(any_)
            if not first:
                ins += [wout, wup, wdown, gain, bias]
                specs += [any_] * 3 + [vmem] * 2
            if not last:
                outs += proj
            if not first:
                outs.append(shape((rows, width), BF16))
            scratch = [dma((6,)), dma((96,))]
            if not first:
                scratch += [pltpu.VMEM((width, width), BF16), pltpu.VMEM((width, ff), BF16),
                            pltpu.VMEM((ff, width), BF16),
                            pltpu.VMEM((4, 2, cols, rows), BF16), pltpu.VMEM((4, 2, 8, rows), F32),
                            dma((4, 2)), dma((4, 2)), dma((2,))]
            if not last:
                scratch += [pltpu.VMEM((width, cols), BF16)] * 3 + [pltpu.VMEM((cols, width), BF16)] * 2
                scratch += [pltpu.VMEM((n_k, rows, width), BF16), pltpu.VMEM((2, 4, rows, width), BF16), dma]
                scratch += [dma((3, 2)), dma((4, 3, 2)), dma((16,)), dma((3, 2)), dma((3,))]
            return pl.pallas_call(
                functools.partial(exchange, l, first, last),
                out_shape=outs, in_specs=specs, out_specs=[vmem] * len(outs), scratch_shapes=scratch,
                compiler_params=pltpu.CompilerParams(
                    collective_id=l, has_side_effects=True, vmem_limit_bytes=28 * 1024 * 1024),
            )(*ins)

        def call_attend(projected):
            return pl.pallas_call(
                attend,
                out_shape=[shape((n_q, cols, rows), BF16), shape((n_q, 8, rows), F32)],
                in_specs=[any_, vmem, vmem, vmem], out_specs=[vmem, vmem],
                scratch_shapes=[
                    pltpu.SMEM((16, 128), jnp.int32), pltpu.SMEM((n_q * n_k + 4 * GROUP + 1,), jnp.int32),
                    pltpu.VMEM((2 * GROUP, 2 * rows, 2 * rows), F32), pltpu.VMEM((2 * GROUP, 1, 2 * rows), F32),
                    pltpu.VMEM((n_q + 1, cols, rows), F32), pltpu.VMEM((n_q + 1, 2, 1, 2 * rows), F32),
                    pltpu.VMEM((n_q + 1, 2, 1, 2 * rows), F32), dma],
                compiler_params=pltpu.CompilerParams(vmem_limit_bytes=28 * 1024 * 1024),
            )(mask, *projected)

        x = pltpu.with_memory_space_constraint(x, pltpu.HBM)
        wqkv = pltpu.with_memory_space_constraint(wqkv, pltpu.HBM)
        projected = call_exchange(0, x, None)
        for l in range(1, layers):
            *projected, x = call_exchange(l, x, call_attend(projected))
        return call_exchange(layers, x, call_attend(projected))[0]

    placed = (P(("row", "col"), None), P(), P(), P(), P(), P(), P(), P())
    return jax.shard_map(
        per_device, mesh=mesh, in_specs=placed, out_specs=P(("row", "col"), None), check_vma=False
    )
```

profile of v0, /device:TPU:1, one launch (start us, length us, event | category | flops | bytes accessed | tf_op | source)
XLA Modules:
  0.0 80.4 jit_solution(449333957517947298)
XLA Ops:
  0.0 0.0 copy-start.3
  0.0 26.5 %shard_map.82 = (bf16[32,128,256]{2,1,0:T(8,128)(2,1)S(1)}, bf16[33,2,144,128]{3,2,1,0:T(8,128)(2,1)S(1)}, bf16[8,2,128,256]{3,2,1,0:T(8,128)(2,1)S(1)}) custom-call(bf16[128,512]{1,0:T(8,128)(2,1)} %refs_0_.3, bf16[2,512,1536]{2,1,0:T(8,128)(2,1)} %refs_3_.2), custom_call_target="tpu_custom_call" | custom-call | tf_op jit(solution)/shard_map/pallas_call | solution.py:490
  26.5 0.0 copy-done.3
  26.5 0.0 copy-start
  26.5 0.0 copy-start.1
  26.5 0.0 copy-start.2
  26.5 0.0 copy-start.4
  26.6 0.0 copy-start.5
  26.6 4.8 %shard_map.83 = (bf16[8,256,128]{2,1,0:T(8,128)(2,1)S(1)}, f32[8,8,128]{2,1,0:T(8,128)S(1)}) custom-call(s32[128,128]{1,0:T(8,128)S(1)} %copy-done.3, bf16[32,128,256]{2,1,0:T(8,128)(2,1)S(1)} %get-tuple-element.16.kbuf, bf16[33,2,144,128]{3,2,1,0:T(8,128)(2,1)S(1)} %get-tuple-element.17.vbuf, bf16[8,2,128,256]{3,2,1,0:T(8,128)(2,1)S(1)} %get-tuple-element.18.qbuf), custom_call_target="tpu_custom_call" | custom-call | tf_op jit(solution)/shard_map/pallas_call | solution.py:498
  31.4 0.0 copy-done
  31.4 0.0 copy-done.1
  31.4 0.0 copy-done.2
  31.4 0.0 copy-done.4
  31.4 0.0 copy-done.5
  31.4 31.2 %shard_map.84 = (bf16[32,128,256]{2,1,0:T(8,128)(2,1)S(1)}, bf16[33,2,144,128]{3,2,1,0:T(8,128)(2,1)S(1)}, bf16[8,2,128,256]{3,2,1,0:T(8,128)(2,1)S(1)}, bf16[128,512]{1,0:T(8,128)(2,1)S(1)}) custom-call(bf16[128,512]{1,0:T(8,128)(2,1)} %refs_0_.3, bf16[8,256,128]{2,1,0:T(8,128)(2,1)S(1)} %get-tuple-element.19.refs_1_, ...), custom_call_target="tpu_custom_call" | custom-call | tf_op jit(solution)/shard_map/pallas_call | solution.py:490
  62.6 4.6 %shard_map.85 = (bf16[8,256,128]{2,1,0:T(8,128)(2,1)S(1)}, f32[8,8,128]{2,1,0:T(8,128)S(1)}) custom-call(s32[128,128]{1,0:T(8,128)S(1)} %copy-done.3, bf16[32,128,256]{2,1,0:T(8,128)(2,1)S(1)} %get-tuple-element.22.kbuf, bf16[33,2,144,128]{3,2,1,0:T(8,128)(2,1)S(1)} %get-tuple-element.23.vbuf, bf16[8,2,128,256]{3,2,1,0:T(8,128)(2,1)S(1)} %get-tuple-element.24.qbuf), custom_call_target="tpu_custom_call" | custom-call | tf_op jit(solution)/shard_map/pallas_call | solution.py:498
  67.3 12.5 %shard_map.86 = bf16[128,512]{1,0:T(8,128)(2,1)S(1)} custom-call(bf16[128,512]{1,0:T(8,128)(2,1)S(1)} %get-tuple-element.21.refs_0_, bf16[8,256,128]{2,1,0:T(8,128)(2,1)S(1)} %get-tuple-element.25.refs_1_, f32[8,8,128]{2,1,0:T(8,128)S(1)} %get-tuple-element.26.refs_2_, bf16[2,512,512]{2,1,0:T(8,128)(2,1)S(1)} %copy-done.2, ...), custom_call_target="tpu_custom_call" | custom-call | tf_op jit(solution)/shard_map/pallas_call | solution.py:490
  79.8 0.7 copy.10
Async XLA Ops:
  0.0 26.5 %copy-start.3 = (s32[128,128]{1,0:T(8,128)S(1)}, s32[128,128]{1,0:T(8,128)}, u32[]{:S(2)}) copy-start(s32[128,128]{1,0:T(8,128)} %mask.3) | copy-start | bytes 196612
  26.5 4.9 %copy-start = (bf16[2,512,1024]{2,1,0:T(8,128)(2,1)S(1)}, bf16[2,512,1024]{2,1,0:T(8,128)(2,1)}, u32[]{:S(2)}) copy-start(bf16[2,512,1024]{2,1,0:T(8,128)(2,1)} %refs_4_.3) | copy-start | bytes 6291460
  26.5 4.9 %copy-start.1 = (bf16[2,1024,512]{2,1,0:T(8,128)(2,1)S(1)}, bf16[2,1024,512]{2,1,0:T(8,128)(2,1)}, u32[]{:S(2)}) copy-start(bf16[2,1024,512]{2,1,0:T(8,128)(2,1)} %refs_5_.3) | copy-start | bytes 6291460
  26.5 4.9 %copy-start.2 = (bf16[2,512,512]{2,1,0:T(8,128)(2,1)S(1)}, bf16[2,512,512]{2,1,0:T(8,128)(2,1)}, u32[]{:S(2)}) copy-start(bf16[2,512,512]{2,1,0:T(8,128)(2,1)} %refs_3_.3) | copy-start | bytes 3145732
  26.5 4.9 %copy-start.4 = (f32[2,2,512]{2,1,0:T(2,128)S(1)}, f32[2,2,512]{2,1,0:T(2,128)}, u32[]{:S(2)}) copy-start(f32[2,2,512]{2,1,0:T(2,128)} %refs_6_.3) | copy-start | bytes 24580
  26.6 4.9 %copy-start.5 = (f32[2,2,512]{2,1,0:T(2,128)S(1)}, f32[2,2,512]{2,1,0:T(2,128)}, u32[]{:S(2)}) copy-start(f32[2,2,512]{2,1,0:T(2,128)} %refs_7_.3) | copy-start | bytes 24580
where the time goes:
time: 80.4 us
  Pallas kernels  79.6 us (99%)
    pallas_call x3, Pallas kernels, call_exchange(): pl.pallas_call(functools.partial(exchange, l, first, last), out_shape=out...  70.2 us
    pallas_call x2, Pallas kernels, call_attend(): pl.pallas_call(attend, out_shape=[shape((n_q, cols, rows), BF16), shape((...  9.45 us

commit v1 on v0

--- a/solution.py
+++ b/solution.py
@@ -14,6 +14,9 @@
 MESH = pl.DeviceIdType.MESH
 OFFS = (0, -1, 1, 2)
 GROUP, AHEAD = 4, 4
+GROUPS = (((0, 0),), ((1, 0),), ((2, 0), (0, 1)), ((0, 2),), ((3, 0),), ((0, 3), (1, 1)),
+          ((1, 2), (2, 1), (2, 2)), ((1, 3), (2, 3)), ((3, 1), (3, 2)), ((3, 3),))
+GROUP_OF = {block: i for i, group in enumerate(GROUPS) for block in group}
 
 
 def layer_norm(values, gain, bias):
@@ -40,7 +43,9 @@
     refs = list(refs)
     take = refs.pop
     x_in = take(0)
-    if not first:
+    if first:
+        mask = take(0)
+    else:
         pin, sin = take(0), take(0)
     hqkv = None if last else take(0)
     if not first:
@@ -49,9 +54,13 @@
         x_out = take(0)
     else:
         kbuf, vbuf, qbuf = take(0), take(0), take(0)
-        if not first:
+        if first:
+            listed = take(0)
+        else:
             x_out = take(0)
     w_sem, snd = take(0), take(0)
+    if first:
+        masked, m_sem = take(0), take(0)
     if not first:
         wout, wup, wdown, rp, rs, er, tr, own_sem = (take(0) for _ in range(8))
     if not last:
@@ -87,20 +96,19 @@
     def nat_partner(ka, kb):
         return bv[ka] * fb + av[kb] * fa
 
-    started = []
 
     def remote(src, dst, send, recv, device):
         return pltpu.make_async_remote_copy(
             src_ref=src, dst_ref=dst, send_sem=send, recv_sem=recv, device_id=device, device_id_type=MESH)
 
-    def go(src, dst, recv, device):
-        copy = remote(src, dst, snd.at[len(started)], recv, device)
-        copy.start()
-        started.append(copy)
+    def go(kind, src, dst, recv, device):
+        remote(src, dst, snd.at[kind], recv, device).start()
 
     if first:
         own = pltpu.make_async_copy(x_in, xk.at[c * 16 + z * 4 + x], x_sem)
         own.start()
+        own_mask = pltpu.make_async_copy(mask, masked, m_sem)
+        own_mask.start()
     loads = []
     if not last:
         for i, dst in enumerate((wq, wk, wv)):
@@ -125,17 +133,17 @@
     pl.semaphore_wait(barrier, len(peers))
 
     if not first:
-        def ret(i, core, src_slot):
-            go(sin.at[src_slot], rs.at[y, c], tr.at[y, c], dev_y(i, core))
-            go(pin.at[src_slot], rp.at[y, c], er.at[y, c], dev_y(i, core))
+        def ret(i, core):
+            src, to = yv[i] * 2 + core, y * 2 + c
+            go(0, sin.at[src], rs.at[to], tr, dev_y(i, core))
+            go(1, pin.at[src], rp.at[to], er, dev_y(i, core))
 
         for i in (3, 1, 2):
             for core in (0, 1):
-                ret(i, core, yv[i] * 2 + core)
-        go(sin.at[y * 2 + e], rs.at[y, c], tr.at[y, c], partner)
-        go(pin.at[y * 2 + e], rp.at[y, c], er.at[y, c], partner)
-        own_s = pltpu.make_async_copy(sin.at[y * 2 + c], rs.at[y, c], own_sem.at[0])
-        own_p = pltpu.make_async_copy(pin.at[y * 2 + c], rp.at[y, c], own_sem.at[1])
+                ret(i, core)
+        ret(0, e)
+        own_s = pltpu.make_async_copy(sin.at[y * 2 + c], rs.at[y * 2 + c], own_sem.at[0])
+        own_p = pltpu.make_async_copy(pin.at[y * 2 + c], rp.at[y * 2 + c], own_sem.at[1])
         own_s.start()
         own_p.start()
 
@@ -158,18 +166,12 @@
         own_s.wait()
         own_p.wait()
 
-        def wait_in(buf, recv, i, core):
-            remote(buf.at[yv[i], core], buf.at[yv[i], core], snd.at[0], recv.at[yv[i], core], partner).wait_recv()
-
-        wait_in(rs, tr, 0, e)
-        wait_in(rp, er, 0, e)
-        for i in (1, 2, 3):
-            for core in (0, 1):
-                wait_in(rs, tr, i, core)
-                wait_in(rp, er, i, core)
+        for buf, recv in ((rs, tr), (rp, er)):
+            ref = buf.at[pl.ds(0, 7)]
+            remote(ref, ref, snd.at[0], recv, partner).wait_recv()
         parts = []
         for g in range(2):
-            stats = [rs[yv[i], g] for i in range(4)]
+            stats = [rs[yv[i] * 2 + g] for i in range(4)]
             top = functools.reduce(jnp.maximum, [t[:4] for t in stats])
             share = [jnp.exp2(t[:4] - top) for t in stats]
             mass = functools.reduce(jnp.add, [f * t[4:] for f, t in zip(share, stats)])
@@ -177,20 +179,24 @@
             share = [f * inverse for f in share]
             for h in range(4):
                 span = slice(h * hd, (h + 1) * hd)
-                total = rp[yv[0], g, span].astype(F32) * share[0][h:h + 1]
+                total = rp[yv[0] * 2 + g, span].astype(F32) * share[0][h:h + 1]
                 for i in (1, 2, 3):
-                    total = total + rp[yv[i], g, span].astype(F32) * share[i][h:h + 1]
+                    total = total + rp[yv[i] * 2 + g, span].astype(F32) * share[i][h:h + 1]
                 parts.append(total)
         attn = jnp.concatenate(parts, axis=0).T.astype(BF16)
-        mixed = jnp.dot(attn, wout[...], preferred_element_type=F32)
-        hidden = layer_norm(x_in[...].astype(F32) + mixed,
-                            gain[l - 1, 0:1], bias[l - 1, 0:1]).astype(BF16)
-        up = gelu(jnp.dot(hidden, wup[...], preferred_element_type=F32)).astype(BF16)
-        down = jnp.dot(up, wdown[...], preferred_element_type=F32)
-        x_new = layer_norm(hidden.astype(F32) + down, gain[l - 1, 1:2], bias[l - 1, 1:2]).astype(BF16)
-        if not last:
-            xk[c * 16 + z * 4 + x] = x_new
-        x_out[...] = x_new
+
+        def finish_layer(span):
+            mixed = jnp.dot(attn[span], wout[...], preferred_element_type=F32)
+            hidden = layer_norm(x_in[span].astype(F32) + mixed, gain[l - 1, 0:1], bias[l - 1, 0:1]).astype(BF16)
+            up = gelu(jnp.dot(hidden, wup[...], preferred_element_type=F32)).astype(BF16)
+            down = jnp.dot(up, wdown[...], preferred_element_type=F32)
+            x_new = layer_norm(hidden.astype(F32) + down, gain[l - 1, 1:2], bias[l - 1, 1:2]).astype(BF16)
+            if not last:
+                xk[c * 16 + z * 4 + x, span] = x_new
+            x_out[span] = x_new
+
+    if last:
+        finish_layer(slice(0, rows))
 
     if not last:
         own_slot = c * 16 + z * 4 + x
@@ -201,39 +207,42 @@
             return ref if h is None else ref.at[pl.ds(h * half, half)]
 
         def arrived(ref, recv):
-            remote(ref, ref, snd.at[0], recv, partner).wait_recv()
+            remote(ref, ref, snd.at[2], recv, partner).wait_recv()
+
+        def sem_at(i, h):
+            return 4 if i == 3 else 2 * (i - 1) + h
 
         def send_a(ka, h, up):
             ref = part(xk.at[c * 16 + nat(ka, 0)], h)
             to = (1 if up else 2) if ka == 0 else 3
-            go(ref, ref, ra.at[to - 1, h], dev_a(2 if up else 1))
-
-        def wait_a(ka, h):
-            arrived(part(xk.at[c * 16 + nat(ka, 0)], h), ra.at[ka - 1, h])
+            go(2, ref, ref, ra.at[sem_at(to, h)], dev_a(2 if up else 1))
+
+        def wait_a(ka, h=None):
+            arrived(part(xk.at[c * 16 + nat(ka, 0)], h), ra.at[sem_at(ka, h)])
 
         def send_b(ka, kb, h, up):
             ref = part(xk.at[c * 16 + nat(ka, kb)], h)
             to = (1 if up else 2) if kb == 0 else 3
-            go(ref, ref, rb.at[ka, to - 1, h], dev_b(2 if up else 1))
-
-        def wait_b(ka, kb, h):
-            arrived(part(xk.at[c * 16 + nat(ka, kb)], h), rb.at[ka, kb - 1, h])
+            go(2, ref, ref, rb.at[ka, sem_at(to, h)], dev_b(2 if up else 1))
+
+        def wait_b(ka, kb, h=None):
+            arrived(part(xk.at[c * 16 + nat(ka, kb)], h), rb.at[ka, sem_at(kb, h)])
 
         def send_y(i, h, up):
             ref = part(xk.at[own_slot] if i == 0 else xq.at[c, yv[i]], h)
             to = (1 if up else 2) if i == 0 else 3
-            go(ref, part(xq.at[c, yv[i]], h), ry.at[to - 1, h], dev_y(2 if up else 1, c))
-
-        def wait_y(i, h):
-            arrived(part(xq.at[c, yv[i]], h), ry.at[i - 1, h])
+            go(3, ref, part(xq.at[c, yv[i]], h), ry.at[sem_at(to, h)], dev_y(2 if up else 1, c))
+
+        def wait_y(i, h=None):
+            arrived(part(xq.at[c, yv[i]], h), ry.at[sem_at(i, h)])
 
         def share(ka, kb):
             n = nat(ka, kb)
-            go(xk.at[c * 16 + n], xk.at[c * 16 + n], rd.at[n], partner)
+            go(2, xk.at[c * 16 + n], xk.at[c * 16 + n], rd.at[GROUP_OF[ka, kb]], partner)
 
         def share_y(i):
             ref = xq.at[c, yv[i]]
-            go(ref, ref, rq.at[i - 1], partner)
+            go(3, ref, ref, rq.at[i - 1], partner)
 
         def project_kv(s, t):
             xs = jnp.concatenate([xk[s], xk[t]], axis=0)
@@ -245,43 +254,46 @@
                 vbuf[to, 0, :2 * hd] = v[:2 * hd, span]
                 vbuf[to, 1, :2 * hd] = v[2 * hd:, span]
 
-        def project_q(q, xs):
+        def project_q(i, mine, other):
+            xs = jnp.concatenate([mine, other], axis=0)
             t = lax.dot_general(wqt[...], xs, (((1,), (1,)), ((), ())), preferred_element_type=F32)
             t = (t * scale).astype(BF16)
-            for h in range(2):
-                base = h * 2 * hd
-                qbuf[q, h, :hd, :rows] = t[base:base + hd]
-                qbuf[q, h, hd:, rows:] = t[base + hd:base + 2 * hd]
+            for j, core in enumerate((c, e)):
+                span = slice(j * rows, (j + 1) * rows)
+                for h in range(2):
+                    base = h * 2 * hd
+                    qbuf[yv[i] * 2 + core, h, :hd, :rows] = t[base:base + hd, span]
+                    qbuf[yv[i] * 2 + core, h, hd:, rows:] = t[base + hd:base + 2 * hd, span]
 
         def finish(*blocks):
+            assert blocks in GROUPS
+            arrived(xk.at[pl.ds(0, len(blocks))], rd.at[GROUPS.index(blocks)])
             for ka, kb in blocks:
-                n, m = nat(ka, kb), nat_partner(ka, kb)
-                s, t = c * 16 + n, e * 16 + m
-                arrived(xk.at[t], rd.at[m])
-                project_kv(s, t)
+                project_kv(c * 16 + nat(ka, kb), e * 16 + nat_partner(ka, kb))
 
         def finish_y(*which):
             for i in which:
                 if i == 0:
-                    project_q(y * 2 + c, xk[own_slot])
-                    project_q(y * 2 + e, xk[e * 16 + z * 4 + x])
-                    continue
-                arrived(xq.at[e, yv[i]], rq.at[i - 1])
-
-                @pl.loop(0, 2)
-                def _(core):
-                    project_q(yv[i] * 2 + core, xq[core, yv[i]])
-
+                    project_q(0, xk[own_slot], xk[e * 16 + z * 4 + x])
+                else:
+                    arrived(xq.at[e, yv[i]], rq.at[i - 1])
+                    project_q(i, xq[c, yv[i]], xq[e, yv[i]])
+
+        def send_own(h, up):
+            send_a(0, h, up)
+            send_b(0, 0, h, up)
+            send_y(0, h, up)
+
+        if not first:
+            finish_layer(slice(0, rows))
         for h in (0, 1):
-            send_a(0, h, True)
-            send_a(0, 1 - h, False)
-            send_b(0, 0, h, True)
-            send_b(0, 0, 1 - h, False)
-            send_y(0, h, True)
-            send_y(0, 1 - h, False)
+            send_own(h, True)
+            send_own(1 - h, False)
         share(0, 0)
         if first:
             project_setup()
+            own_mask.wait()
+            link_pairs(masked, listed)
         finish((0, 0))
         finish_y(0)
         wait_a(1, 0)
@@ -317,9 +329,8 @@
         wait_y(2, 0)
         share_y(2)
         finish((1, 0))
-        wait_a(3, 0)
+        wait_a(3)
         send_b(3, 0, 0, True)
-        wait_a(3, 1)
         send_b(3, 0, 1, False)
         send_b(3, 0, 1, True)
         send_b(3, 0, 0, False)
@@ -330,8 +341,7 @@
             send_b(ka, 1, 0, True)
             wait_b(ka, 2, 1)
             send_b(ka, 2, 1, False)
-        wait_b(0, 3, 0)
-        wait_b(0, 3, 1)
+        wait_b(0, 3)
         share(0, 3)
         finish((0, 2))
         finish_y(1, 2)
@@ -340,8 +350,7 @@
             share(ka, 1)
             wait_b(ka, 2, 0)
             share(ka, 2)
-        wait_y(3, 0)
-        wait_y(3, 1)
+        wait_y(3)
         share_y(3)
         finish((3, 0))
         wait_b(3, 1, 0)
@@ -350,8 +359,7 @@
         send_b(3, 2, 1, False)
         finish((0, 3), (1, 1))
         for ka in (1, 2):
-            wait_b(ka, 3, 0)
-            wait_b(ka, 3, 1)
+            wait_b(ka, 3)
             share(ka, 3)
         wait_b(3, 1, 1)
         share(3, 1)
@@ -360,48 +368,79 @@
         finish((1, 2), (2, 1), (2, 2))
         finish_y(3)
         finish((1, 3), (2, 3))
-        wait_b(3, 3, 0)
-        wait_b(3, 3, 1)
+        wait_b(3, 3)
         share(3, 3)
-        finish((3, 1), (3, 2), (3, 3))
-
-    for copy in started:
-        copy.wait_send()
-
-
-def attend(mask, kbuf, vbuf, qbuf, pout, sout, smask, pairs, sbuf, peak, acc, top, den, sem):
-    n_q, n_k, rows = qbuf.shape[0], kbuf.shape[0], kbuf.shape[1]
+        finish((3, 1), (3, 2))
+        finish((3, 3))
+
+    kinds = []
+    if not first:
+        kinds += [(0, sin.at[pl.ds(0, 7)]), (1, pin.at[pl.ds(0, 7)])]
+    if not last:
+        kinds += [(2, xk.at[pl.ds(0, 31)]), (3, xk.at[pl.ds(0, 6)])]
+    for kind, ref in kinds:
+        remote(ref, ref, snd.at[kind], er if not first else rq.at[0], partner).wait_send()
+
+
+def link_pairs(mask, out):
+    x, y, z, c = coords()
+    n_q, n_k = 8, 32
+    lane = lax.broadcasted_iota(jnp.int32, (1, 128), 1)
+    in_row, of_row = lane & 15, lane >> 4
+    slot = (in_row & 1) * 16 + (of_row >> 1) * 4 + (of_row & 1) * 2 + ((in_row >> 1) & 1)
+    slot = slot.astype(F32)
+    base = lax.axis_index("row") * 16 + (x % 2) * 2
+    linked = [jnp.where((in_row >> 2) == y, mask[pl.ds(base + (q // 2) * 4 + q % 2, 1), :], 0).astype(F32)
+              for q in range(n_q)]
+    upper = lax.broadcasted_iota(jnp.int32, (128, 128), 0) < lax.broadcasted_iota(jnp.int32, (128, 128), 1)
+    rank = jnp.dot(jnp.concatenate(linked, axis=0).astype(BF16), jnp.where(upper, 1.0, 0.0).astype(BF16),
+                   preferred_element_type=F32)
+    start = jnp.zeros((1, 1), F32)
+    places, pads = [], []
+    for q in range(n_q):
+        code = slot + float(q * n_k)
+        count = jnp.sum(linked[q], axis=1, keepdims=True)
+        odd = count - 2.0 * jnp.floor(count * 0.5)
+        places.append(jnp.where(linked[q] > 0.0, rank[q:q + 1] + start, -1.0))
+        pads.append((start + count, odd, jnp.max(jnp.where(linked[q] > 0.0, code, 0.0), axis=1, keepdims=True)))
+        start = start + count + odd
+    places = jnp.concatenate(places + [jnp.zeros((120, 128), F32)], axis=0).T
+    for chunk in range(3):
+        at = (lane + chunk * 128).astype(F32)
+        code = jnp.zeros((1, 128), F32)
+        filler = jnp.zeros((1, 128), F32)
+        for q in range(n_q):
+            hot = jnp.where(places[:, q:q + 1] == at, 1.0, 0.0).astype(BF16)
+            codes = jnp.broadcast_to(slot + float(q * n_k), (8, 128)).astype(BF16)
+            where, odd, last = pads[q]
+            pad = jnp.where(at == where, odd, 0.0)
+            code = code + jnp.dot(codes, hot, preferred_element_type=F32)[0:1] + pad * last
+            filler = filler + pad
+        code = code.astype(jnp.int32)
+        key = code & 31
+        entry = (code >> 5) * 4096 + key * 64 + jnp.where(filler > 0.0, n_k, key)
+        out[chunk:chunk + 1, :] = jnp.where(at < start, entry, n_q * 4096 + n_k)
+    out[3:4, :] = jnp.broadcast_to(start, (1, 128)).astype(jnp.int32)
+
+
+def attend(listed, kbuf, vbuf, qbuf, pout, sout, pairs, sbuf, peak, acc, top, den, sem):
+    n_q, rows = qbuf.shape[0], kbuf.shape[1]
     hd = qbuf.shape[2] // 2
-    x, y, z, c = coords()
-    row = lax.axis_index("row")
-    load = pltpu.make_async_copy(mask.at[pl.ds(row * 16, 16)], smask, sem)
+    load = pltpu.make_async_copy(listed, pairs, sem)
     load.start()
     acc[...] = jnp.zeros_like(acc)
     den[...] = jnp.zeros_like(den)
     top[...] = jnp.full_like(top, FLOOR)
     load.wait()
-
-    def scan(q, n):
-        at = (q // 2) * 4 + (x % 2) * 2 + q % 2
-        base = q * 4096
-        for s in range(n_k):
-            core, zz, xx = s // 16, (s % 16) // 4, s % 4
-            kid = (zz * 2 + xx // 2) * 16 + y * 4 + (xx % 2) * 2 + core
-            pairs[n] = base + (s * 64 + s)
-            n = n + smask[at, kid]
-        before = pairs[jnp.maximum(n - 1, 0)]
-        pairs[n] = (before // 64) * 64 + n_k
-        return n + n % 2
-
-    n = lax.fori_loop(0, n_q, scan, 0)
-    for i in range(4 * GROUP):
-        pairs[n + i] = n_q * 4096 + n_k
-
+    n = pairs[3, 0]
     units = 2 * GROUP
+
+    def entry(i):
+        return pairs[i // 128, i % 128]
 
     def scores(it, i):
         d, h = i // 2, i % 2
-        code = [pairs[(it * GROUP + d) * 2 + j] for j in range(2)]
+        code = [entry((it * GROUP + d) * 2 + j) for j in range(2)]
         q = jnp.minimum(code[0] // 4096, n_q - 1)
         best = []
         for j in range(2):
@@ -413,7 +452,7 @@
 
     def values(it, i):
         d, h = i // 2, i % 2
-        code = [pairs[(it * GROUP + d) * 2 + j] for j in range(2)]
+        code = [entry((it * GROUP + d) * 2 + j) for j in range(2)]
         q = code[0] // 4096
         old = top[q, h]
         new = jnp.maximum(old, peak[i])
@@ -464,7 +503,10 @@
         def call_exchange(l, x, part):
             first, last = l == 0, l == layers
             ins, specs, outs = [x], [any_ if first else vmem], []
-            if not first:
+            if first:
+                ins.append(mask)
+                specs.append(any_)
+            else:
                 ins += part
                 specs += [vmem, vmem]
             if not last:
@@ -475,18 +517,22 @@
                 specs += [any_] * 3 + [vmem] * 2
             if not last:
                 outs += proj
-            if not first:
+            if first:
+                outs.append(shape((8, 128), jnp.int32))
+            else:
                 outs.append(shape((rows, width), BF16))
-            scratch = [dma((6,)), dma((96,))]
+            scratch = [dma((6,)), dma((4,))]
+            if first:
+                scratch += [pltpu.VMEM((128, 128), jnp.int32), dma]
             if not first:
                 scratch += [pltpu.VMEM((width, width), BF16), pltpu.VMEM((width, ff), BF16),
                             pltpu.VMEM((ff, width), BF16),
-                            pltpu.VMEM((4, 2, cols, rows), BF16), pltpu.VMEM((4, 2, 8, rows), F32),
-                            dma((4, 2)), dma((4, 2)), dma((2,))]
+                            pltpu.VMEM((8, cols, rows), BF16), pltpu.VMEM((8, 8, rows), F32),
+                            dma, dma, dma((2,))]
             if not last:
                 scratch += [pltpu.VMEM((width, cols), BF16)] * 3 + [pltpu.VMEM((cols, width), BF16)] * 2
                 scratch += [pltpu.VMEM((n_k, rows, width), BF16), pltpu.VMEM((2, 4, rows, width), BF16), dma]
-                scratch += [dma((3, 2)), dma((4, 3, 2)), dma((16,)), dma((3, 2)), dma((3,))]
+                scratch += [dma((5,)), dma((4, 5)), dma((len(GROUPS),)), dma((5,)), dma((3,))]
             return pl.pallas_call(
                 functools.partial(exchange, l, first, last),
                 out_shape=outs, in_specs=specs, out_specs=[vmem] * len(outs), scratch_shapes=scratch,
@@ -494,25 +540,26 @@
                     collective_id=l, has_side_effects=True, vmem_limit_bytes=28 * 1024 * 1024),
             )(*ins)
 
-        def call_attend(projected):
+        def call_attend(listed, projected):
             return pl.pallas_call(
                 attend,
                 out_shape=[shape((n_q, cols, rows), BF16), shape((n_q, 8, rows), F32)],
-                in_specs=[any_, vmem, vmem, vmem], out_specs=[vmem, vmem],
+                in_specs=[vmem] * 4, out_specs=[vmem, vmem],
                 scratch_shapes=[
-                    pltpu.SMEM((16, 128), jnp.int32), pltpu.SMEM((n_q * n_k + 4 * GROUP + 1,), jnp.int32),
+                    pltpu.SMEM((8, 128), jnp.int32),
                     pltpu.VMEM((2 * GROUP, 2 * rows, 2 * rows), F32), pltpu.VMEM((2 * GROUP, 1, 2 * rows), F32),
                     pltpu.VMEM((n_q + 1, cols, rows), F32), pltpu.VMEM((n_q + 1, 2, 1, 2 * rows), F32),
                     pltpu.VMEM((n_q + 1, 2, 1, 2 * rows), F32), dma],
                 compiler_params=pltpu.CompilerParams(vmem_limit_bytes=28 * 1024 * 1024),
-            )(mask, *projected)
+            )(listed, *projected)
 
         x = pltpu.with_memory_space_constraint(x, pltpu.HBM)
         wqkv = pltpu.with_memory_space_constraint(wqkv, pltpu.HBM)
-        projected = call_exchange(0, x, None)
+        mask = pltpu.with_memory_space_constraint(mask, pltpu.HBM)
+        *projected, listed = call_exchange(0, x, None)
         for l in range(1, layers):
-            *projected, x = call_exchange(l, x, call_attend(projected))
-        return call_exchange(layers, x, call_attend(projected))[0]
+            *projected, x = call_exchange(l, x, call_attend(listed, projected))
+        return call_exchange(layers, x, call_attend(listed, projected))[0]
 
     placed = (P(("row", "col"), None), P(), P(), P(), P(), P(), P(), P())
     return jax.shard_map(

time: 80.4 us -> 75 us (0.933); the launches traced: 80.4 us -> 73.9 us
  Pallas kernels: 79.6 us -> 73.1 us
    pallas_call x2, Pallas kernels: 9.45 us -> 5.89 us  [call_attend(): pl.pallas_call(attend, out_shape=[shape((n_q, cols, rows), BF16), shape((...]
    pallas_call x3, Pallas kernels: 70.2 us -> 67.2 us  [call_exchange(): pl.pallas_call(functools.partial(exchange, l, first, last), out_shape=out...]
where the time goes in v1:
time: 75 us; the launch traced here: 73.9 us
  Pallas kernels  73.1 us (97%)
    pallas_call x3, Pallas kernels, call_exchange(): pl.pallas_call(functools.partial(exchange, l, first, last), out_shape=out...  67.2 us
    pallas_call x2, Pallas kernels, call_attend(): pl.pallas_call(attend, out_shape=[shape((n_q, cols, rows), BF16), shape((...  5.89 us

profile of v1, /device:TPU:1, one launch (start us, length us, event | category | flops | bytes accessed | tf_op | source)
XLA Modules:
  0.0 73.9 jit_solution(6460465649417322150)
XLA Ops:
  0.0 24.8 %shard_map.82 = (bf16[32,128,256]{2,1,0:T(8,128)(2,1)S(1)}, bf16[33,2,144,128]{3,2,1,0:T(8,128)(2,1)S(1)}, bf16[8,2,128,256]{3,2,1,0:T(8,128)(2,1)S(1)}, s32[8,128]{1,0:T(8,128)S(1)}) custom-call(bf16[128,512]{1,0:T(8,128)(2,1)} %refs_0_.3, s32[128,128]{1,0:T(8,128)} %refs_1_.1, bf16[2,512,1536]{2,1,0:T(8,128)(2,1)} %refs_3_.2), custom_call_target="tpu_custom_call" | custom-call | tf_op jit(solution)/shard_map/pallas_call | solution.py:536
  24.8 0.0 copy-start
  24.8 0.0 copy-start.1
  24.8 0.0 copy-start.2
  24.8 0.0 copy-start.3
  24.8 0.0 copy-start.4
  24.8 2.9 %shard_map.83 = (bf16[8,256,128]{2,1,0:T(8,128)(2,1)S(1)}, f32[8,8,128]{2,1,0:T(8,128)S(1)}) custom-call(s32[8,128]{1,0:T(8,128)S(1)} %get-tuple-element.17.listed, bf16[32,128,256]{2,1,0:T(8,128)(2,1)S(1)} %get-tuple-element.18.kbuf, bf16[33,2,144,128]{3,2,1,0:T(8,128)(2,1)S(1)} %get-tuple-element.19.vbuf, bf16[8,2,128,256]{3,2,1,0:T(8,128)(2,1)S(1)} %get-tuple-element.20.qbuf), custom_call_target="tpu_custom_call" | custom-call | tf_op jit(solution)/shard_map/pallas_call | solution.py:544
  27.8 0.0 copy-done
  27.8 0.0 copy-done.1
  27.8 0.0 copy-done.2
  27.8 0.0 copy-done.3
  27.8 0.0 copy-done.4
  27.8 30.6 %shard_map.84 = (bf16[32,128,256]{2,1,0:T(8,128)(2,1)S(1)}, bf16[33,2,144,128]{3,2,1,0:T(8,128)(2,1)S(1)}, bf16[8,2,128,256]{3,2,1,0:T(8,128)(2,1)S(1)}, bf16[128,512]{1,0:T(8,128)(2,1)S(1)}) custom-call(bf16[128,512]{1,0:T(8,128)(2,1)} %refs_0_.3, bf16[8,256,128]{2,1,0:T(8,128)(2,1)S(1)} %get-tuple-element.21.refs_1_, ...), custom_call_target="tpu_custom_call" | custom-call | tf_op jit(solution)/shard_map/pallas_call | solution.py:536
  58.5 3.0 %shard_map.85 = (bf16[8,256,128]{2,1,0:T(8,128)(2,1)S(1)}, f32[8,8,128]{2,1,0:T(8,128)S(1)}) custom-call(s32[8,128]{1,0:T(8,128)S(1)} %get-tuple-element.17.listed, bf16[32,128,256]{2,1,0:T(8,128)(2,1)S(1)} %get-tuple-element.24.kbuf, bf16[33,2,144,128]{3,2,1,0:T(8,128)(2,1)S(1)} %get-tuple-element.25.vbuf, bf16[8,2,128,256]{3,2,1,0:T(8,128)(2,1)S(1)} %get-tuple-element.26.qbuf), custom_call_target="tpu_custom_call" | custom-call | tf_op jit(solution)/shard_map/pallas_call | solution.py:544
  61.4 11.8 %shard_map.86 = bf16[128,512]{1,0:T(8,128)(2,1)S(1)} custom-call(bf16[128,512]{1,0:T(8,128)(2,1)S(1)} %get-tuple-element.23.refs_0_, bf16[8,256,128]{2,1,0:T(8,128)(2,1)S(1)} %get-tuple-element.27.refs_1_, f32[8,8,128]{2,1,0:T(8,128)S(1)} %get-tuple-element.28.refs_2_, bf16[2,512,512]{2,1,0:T(8,128)(2,1)S(1)} %copy-done.2, ...), custom_call_target="tpu_custom_call" | custom-call | tf_op jit(solution)/shard_map/pallas_call | solution.py:536
  73.3 0.7 copy.10
Async XLA Ops:
  24.8 3.0 %copy-start = (bf16[2,512,1024]{2,1,0:T(8,128)(2,1)S(1)}, bf16[2,512,1024]{2,1,0:T(8,128)(2,1)}, u32[]{:S(2)}) copy-start(bf16[2,512,1024]{2,1,0:T(8,128)(2,1)} %refs_4_.3) | copy-start | bytes 6291460
  24.8 3.0 %copy-start.1 = (bf16[2,1024,512]{2,1,0:T(8,128)(2,1)S(1)}, bf16[2,1024,512]{2,1,0:T(8,128)(2,1)}, u32[]{:S(2)}) copy-start(bf16[2,1024,512]{2,1,0:T(8,128)(2,1)} %refs_5_.3) | copy-start | bytes 6291460
  24.8 3.0 %copy-start.2 = (bf16[2,512,512]{2,1,0:T(8,128)(2,1)S(1)}, bf16[2,512,512]{2,1,0:T(8,128)(2,1)}, u32[]{:S(2)}) copy-start(bf16[2,512,512]{2,1,0:T(8,128)(2,1)} %refs_3_.3) | copy-start | bytes 3145732
  24.8 3.0 %copy-start.3 = (f32[2,2,512]{2,1,0:T(2,128)S(1)}, f32[2,2,512]{2,1,0:T(2,128)}, u32[]{:S(2)}) copy-start(f32[2,2,512]{2,1,0:T(2,128)} %refs_6_.3) | copy-start | bytes 24580
  24.8 3.0 %copy-start.4 = (f32[2,2,512]{2,1,0:T(2,128)S(1)}, f32[2,2,512]{2,1,0:T(2,128)}, u32[]{:S(2)}) copy-start(f32[2,2,512]{2,1,0:T(2,128)} %refs_7_.3) | copy-start | bytes 24580
